TPU v7x, 32 devices: a whole 2x2x4 slice. The times are simulated.
32 devices in a mesh: row: 8 (over y, x, core), shift: 4 (over z).
Axes of the slice: x: 2, y: 2, z: 4, core: 2. Of those that a mesh axis runs over, the one named last changes fastest.
Arguments:
- snapshots: bfloat16 [4096, 2, 128], P('row'), may hold values from -6 to 6
- tail_sensors: bfloat16 [128, 2, 128], replicated, may hold values from -6 to 6
- shift_offsets: int32 [12], P('shift'), may hold values from 0 to 128
- start_basis: float32 [64, 4096], P(None, 'row'), may hold values from -0.09375 to 0.09375
Outputs:
- covariance: float32 [4096, 4096], P('row', 'shift')
- signal_basis: float32 [64, 4096], P(None, 'row')
Inputs may be any that keep to these rules, and one draw needn't show every extreme that they name: `shift_offsets`: each shift's first sensor.
All inputs are finite; a program needn't handle non-finite values.
Results may differ from a plain program's by a relative error of at most 0.0031.
Values may be sent and summed in bfloat16 or wider, within the bound.
A program may use at most 64 MiB of HBM per device.

v0:
```python
import jax
import jax.numpy as jnp
from jax import lax
from jax.sharding import PartitionSpec as P

M = 4096
SNAPS = 128
ITERS = 2
half_root = 0.7071067811865476


def make_some(extended, offset, start, count):
    window = lax.dynamic_slice_in_dim(extended, offset + start, count, 0).astype(jnp.float32)
    mirror = lax.dynamic_slice_in_dim(extended, offset + M - start - count, count, 0).astype(
        jnp.float32
    )[::-1]
    summed_pair = window + mirror
    difference = window - mirror
    upper_rows = jnp.concatenate([summed_pair[:, 0], summed_pair[:, 1]], axis=1)
    bottom = jnp.concatenate([difference[:, 1], -difference[:, 0]], axis=1)
    positions = start + jnp.arange(count, dtype=jnp.int32)
    chosen = jnp.where((positions < M // 2)[:, None], upper_rows, bottom)
    return (chosen * half_root).astype(jnp.bfloat16)


def factor(gram_matrix):
    lower_factor = jnp.linalg.cholesky(gram_matrix)
    identity = jnp.eye(gram_matrix.shape[0], dtype=jnp.float32)
    return jax.scipy.linalg.solve_triangular(lower_factor, identity, lower=True)


def per_device(snapshots, tail_sensors, shift_offsets, start_basis):
    block_rows = snapshots.shape[0]
    row_index = lax.axis_index("row")
    shift_index = lax.axis_index("shift")
    col_count = M // lax.axis_size("shift")
    normalizer = 1.0 / (SNAPS * shift_offsets.shape[0] * lax.axis_size("shift"))
    gathered = lax.all_gather(snapshots, "row", axis=0, tiled=True)
    extended = jnp.concatenate([gathered, tail_sensors], 0)
    every_offset = lax.all_gather(shift_offsets, "shift", axis=0, tiled=True)
    row_start = row_index * block_rows
    col_start = shift_index * col_count

    def add_block(which, running):
        offset = every_offset[which]
        own_rows = make_some(extended, offset, row_start, block_rows)
        col_rows = make_some(extended, offset, col_start, col_count)
        return running + lax.dot_general(
            own_rows, col_rows, (((1,), (1,)), ((), ())), preferred_element_type=jnp.float32
        )

    summed_block = lax.fori_loop(
        0, every_offset.shape[0], add_block, jnp.zeros((block_rows, col_count), jnp.float32)
    )
    cov_out = summed_block * normalizer
    basis_rows = lax.all_gather(start_basis, "row", axis=1, tiled=True)
    own_basis = start_basis
    for sweep in range(ITERS):
        basis_cols = lax.dynamic_slice_in_dim(basis_rows, shift_index * col_count, col_count, 1)
        column_terms = lax.dot_general(
            basis_cols, cov_out, (((1,), (1,)), ((), ())), precision=lax.Precision.HIGHEST
        )
        mapped = lax.psum(column_terms, "shift")
        local_gram = jnp.dot(mapped, mapped.T, precision=lax.Precision.HIGHEST)
        gram_matrix = lax.psum(local_gram, "row")
        own_basis = jnp.dot(factor(gram_matrix), mapped, precision=lax.Precision.HIGHEST)
        if sweep + 1 < ITERS:
            basis_rows = lax.all_gather(own_basis, "row", axis=1, tiled=True)
    return (cov_out, own_basis)


def solution(mesh):
    in_specs = (P("row", None, None), P(), P("shift"), P(None, "row"))
    out_specs = (P("row", "shift"), P(None, "row"))
    return jax.shard_map(
        per_device, mesh=mesh, in_specs=in_specs, out_specs=out_specs, check_vma=False
    )
```

profile of v0, /device:TPU:0, one launch (start us, length us, event | category | flops | bytes accessed | tf_op | source)
XLA Modules:
  0.0 375.3 jit_solution(9196168970584460465)
XLA Ops:
  8.7 1.3 dynamic-slice
  11.5 9.9 %all-reduce = s32[12]{0:T(128)S(1)} all-reduce(s32[12]{0:T(128)S(1)} %dynamic-update-slice.2), channel_id=1, replica_groups=mesh['row'=8,'shift'=4] {'shift'}, use_global_device_ids=true, to_apply=%add | all-reduce | flops 12 | bytes 96
  21.4 19.0 %all-gather.4.cloned.1.call-done = bf16[4096,2,128]{2,1,0:T(2,128)(2,1)} async-done(((bf16[512,2,128]{2,1,0:T(2,128)(2,1)}), bf16[4096,2,128]{2,1,0:T(2,128)(2,1)}) %all-gather.4.cloned.1.call-update) | async-done | bytes 2097168 | tf_op jit(solution)/shard_map/all_gather | solution.py:38
  40.4 6.4 %pad_maximum_fusion = bf16[4224,2,128]{2,1,0:T(2,128)(2,1)S(1)} fusion(bf16[128,2,128]{2,1,0:T(2,128)(2,1)} %param.10, bf16[4096,2,128]{2,1,0:T(2,128)(2,1)} %all-gather.4.cloned.1.call-done), kind=kLoop, calls=%fused_computation.31 | loop fusion | flops 1081344 | bytes 4325376 | tf_op jit(solution)/shard_map/concatenate | solution.py:39
  46.8 1.6 copy.30
  48.4 143.1 %while.18 = (s32[]{:T(128)}, f32[512,1024]{1,0:T(8,128)}, s32[]{:T(128)}, s32[12]{0:T(128)S(1)}, bf16[4224,2,128]{2,0,1:T(8,128)(2,1)}, /*index=5*/s32[]{:T(128)...) while((s32[]{:T(128)}, f32[512,1024]{1,0:T(8,128)}, ...), condition=%wide.region_1.2_spmd.clone, body=%wide.region_0.1_spmd.clone.sunk | while | flops 273222688 | bytes 47713820 | solution.py:52
  52.0 1.2 convert_subtract_fusion.4
  59.1 1.3 copy-done.1
  63.9 1.2 convert_subtract_fusion.4
  65.2 1.2 slice_bitcast_fusion.8
  71.0 1.3 copy-done.1
  75.8 1.2 convert_subtract_fusion.4
  77.1 1.2 slice_bitcast_fusion.8
  82.9 1.3 copy-done.1
  87.8 1.2 convert_subtract_fusion.4
  94.9 1.3 copy-done.1
  99.7 1.2 convert_subtract_fusion.4
  106.8 1.3 copy-done.1
  111.6 1.2 convert_subtract_fusion.4
  118.7 1.3 copy-done.1
  123.5 1.2 convert_subtract_fusion.4
  130.6 1.3 copy-done.1
  135.5 1.2 convert_subtract_fusion.4
  142.6 1.3 copy-done.1
  147.4 1.2 convert_subtract_fusion.4
  154.5 1.3 copy-done.1
  159.3 1.2 convert_subtract_fusion.4
  166.4 1.3 copy-done.1
  171.2 1.2 convert_subtract_fusion.4
  178.3 1.3 copy-done.1
  183.2 1.2 convert_subtract_fusion.4
  190.3 1.3 copy-done.1
  191.6 1.8 broadcast_multiply_fusion
  193.4 4.0 %fusion.16 = f32[64,512]{1,0:T(8,128)} fusion(f32[512,1024]{1,0:T(8,128)S(1)} %broadcast_multiply_fusion, f32[64,4096]{1,0:T(8,128)} %all-gather.6.cloned.1.call-done, s32[]{:T(128)S(6)} %select_n.96), kind=kOutput, calls=%fused_computation.35 | convolution fusion | flops 402653184 | bytes 2490372 | tf_op jit(solution)/shard_map/dot_general | solution.py:60
  197.5 34.7 %all-reduce.4.cloned.1.call-done = f32[64,512]{1,0:T(8,128)} async-done(((f32[64,512]{1,0:T(8,128)}), f32[64,512]{1,0:T(8,128)}) %all-reduce.4.cloned.1.call-update) | async-done | bytes 131088 | tf_op jit(solution)/shard_map/psum | solution.py:63
  232.2 1.2 fusion.32
  233.4 22.4 %psum.29 = f32[64,64]{0,1:T(8,128)S(1)} all-reduce(f32[64,64]{0,1:T(8,128)S(1)} %fusion.32), channel_id=1, replica_groups=mesh['row'=8,'shift'=4] {'row'}, use_global_device_ids=true, to_apply=%region_3.4 | all-reduce | flops 4096 | bytes 32768 | tf_op jit(solution)/shard_map/psum | solution.py:65
  255.9 5.8 %cholesky.44 = f32[64,64]{1,0:T(8,128)S(1)} custom-call(f32[64,64]{1,0:T(8,128)S(1)} %fusion.27), custom_call_target="Cholesky" | custom-call | tf_op jit(solution)/shard_map/jit(cholesky)/cholesky | solution.py:27
  263.1 4.9 %custom-call.7 = f32[1,64,64]{1,2,0:T(8,128)S(1)} custom-call(f32[1,64,64]{2,1,0:T(8,128)S(1)} %fusion.22), custom_call_target="InvertDiagBlocksLowerTriangular" | custom-call | tf_op jit(solution)/shard_map/jit(_solve_triangular)/triangular_solve | solution.py:29
  268.2 1.8 fusion.33
  270.1 22.3 %all-gather.8.cloned.1.call-done = f32[64,4096]{1,0:T(8,128)} async-done(((f32[64,512]{1,0:T(8,128)}), f32[64,4096]{1,0:T(8,128)}) %all-gather.8.cloned.1.call-update) | async-done | bytes 1048592 | tf_op jit(solution)/shard_map/all_gather | solution.py:68
  292.4 3.7 fusion.14
  296.2 34.8 %all-reduce.6.cloned.1.call-done = f32[64,512]{1,0:T(8,128)} async-done(((f32[64,512]{1,0:T(8,128)}), f32[64,512]{1,0:T(8,128)}) %all-reduce.6.cloned.1.call-update) | async-done | bytes 131088 | tf_op jit(solution)/shard_map/psum | solution.py:63
  331.0 1.2 fusion.34
  332.2 22.4 %psum.31 = f32[64,64]{0,1:T(8,128)S(1)} all-reduce(f32[64,64]{0,1:T(8,128)S(1)} %fusion.34), channel_id=1, replica_groups=mesh['row'=8,'shift'=4] {'row'}, use_global_device_ids=true, to_apply=%region_7.10 | all-reduce | flops 4096 | bytes 32768 | tf_op jit(solution)/shard_map/psum | solution.py:65
  354.6 5.8 %cholesky.55 = f32[64,64]{1,0:T(8,128)S(1)} custom-call(f32[64,64]{1,0:T(8,128)S(1)} %fusion.25), custom_call_target="Cholesky" | custom-call | tf_op jit(solution)/shard_map/jit(cholesky)/cholesky | solution.py:27
  361.8 4.9 %custom-call.8 = f32[1,64,64]{1,2,0:T(8,128)S(1)} custom-call(f32[1,64,64]{2,1,0:T(8,128)S(1)} %fusion.23), custom_call_target="InvertDiagBlocksLowerTriangular" | custom-call | tf_op jit(solution)/shard_map/jit(_solve_triangular)/triangular_solve | solution.py:29
  367.0 1.8 fusion.35
  (266 shorter events, 89.9 us)
Async XLA Ops:
  7.2 33.2 %all-gather.4.cloned.1.call-start = ((), (), s32[]{:S(2)}) async-start(), calls=%async_computation | async-start | bytes 2359296 | tf_op jit(solution)/shard_map/all_gather | solution.py:38
  7.9 185.5 %all-gather.6.cloned.1.call-start = ((), (), s32[]{:S(2)}) async-start(), calls=%async_computation.1 | async-start | bytes 1179648 | tf_op jit(solution)/shard_map/all_gather | solution.py:56
  8.6 223.5 %all-reduce.4.cloned.1.call-start = ((), (), s32[]{:S(2)}) async-start(), calls=%async_computation.2 | async-start | bytes 262144 | tf_op jit(solution)/shard_map/psum | solution.py:63
  55.7 2.1 copy-start
  56.5 1.4 copy-start.3
  56.5 1.6 copy-start.4
  59.1 1.3 copy-start.1
  67.6 2.1 copy-start
  68.4 1.4 copy-start.3
  68.4 1.6 copy-start.4
  71.0 1.3 copy-start.1
  79.5 2.1 copy-start
  80.4 1.4 copy-start.3
  80.4 1.6 copy-start.4
  82.9 1.3 copy-start.1
  91.5 2.1 copy-start
  92.3 1.4 copy-start.3
  92.3 1.6 copy-start.4
  94.8 1.3 copy-start.1
  103.4 2.1 copy-start
  104.2 1.4 copy-start.3
  104.2 1.6 copy-start.4
  106.8 1.3 copy-start.1
  115.3 2.1 copy-start
  116.1 1.4 copy-start.3
  116.1 1.6 copy-start.4
  118.7 1.3 copy-start.1
  127.2 2.1 copy-start
  128.1 1.4 copy-start.3
  128.1 1.6 copy-start.4
  139.2 2.1 copy-start
  140.0 1.4 copy-start.3
  140.0 1.6 copy-start.4
  151.1 2.1 copy-start
  151.9 1.4 copy-start.3
  151.9 1.6 copy-start.4
  163.0 2.1 copy-start
  163.8 1.4 copy-start.3
  163.8 1.6 copy-start.4
  174.9 2.1 copy-start
  175.8 1.4 copy-start.3
  175.8 1.6 copy-start.4
  186.9 2.1 copy-start
  187.7 1.4 copy-start.3
  187.7 1.6 copy-start.4
  193.4 102.8 %copy-start.5 = (f32[512,1024]{1,0:T(8,128)}, f32[512,1024]{1,0:T(8,128)S(1)}, u32[]{:S(2)}) copy-start(f32[512,1024]{1,0:T(8,128)S(1)} %broadcast_multiply_fusion) | copy-start | bytes 6291460
  197.4 95.0 %all-gather.8.cloned.1.call-start = ((), (), s32[]{:S(2)}) async-start(), calls=%async_computation.3 | async-start | bytes 1179648 | tf_op jit(solution)/shard_map/all_gather | solution.py:68
  270.1 60.9 %all-reduce.6.cloned.1.call-start = ((), (), s32[]{:S(2)}) async-start(), calls=%async_computation.4 | async-start | bytes 262144 | tf_op jit(solution)/shard_map/psum | solution.py:63
  (18 other events, 23.6 us)
Sparse Core Ops, SparseCore 0:
  9.9 30.4 all-gather.3
  42.3 23.3 all-gather.5
  197.5 34.6 all-reduce.3
  270.2 22.1 all-gather.7
  296.3 34.6 all-reduce.5
where the time goes:
time: 378 us; the launch traced here: 375 us
  waiting for transfers between devices  112 us (30%)
  other arithmetic  102 us (27%)
  blocking collectives  54.6 us (14%)
  local copies, waits for them, and re-layouts  39.1 us (10%)
  loops' own time  26.2 us (7%)
  matrix products  26 us (7%)
  between operations  14.5 us (4%)
    psum x2, waiting for transfers between devices, per_device(): mapped = lax.psum(column_terms, 'shift')  69.5 us
    psum x2, blocking collectives, per_device(): gram_matrix = lax.psum(local_gram, 'row')  44.7 us
    sub x24, other arithmetic, make_some(): difference = window - mirror  28.7 us
    another operation x1, loops' own time, per_device(): lax.fori_loop(0, every_offset.shape[0], add_block, jnp.zeros((block_rows,...  26.2 us
    convert_element_type x24, other arithmetic, make_some(): lax.dynamic_slice_in_dim(extended, offset + M - start - count, count, 0)  26 us
    all_gather x1, waiting for transfers between devices, per_device(): basis_rows = lax.all_gather(own_basis, 'row', axis=1, tiled=True)  22.3 us
    while x120, local copies, waits for them, and re-layouts  19.4 us
    all_gather x1, waiting for transfers between devices, per_device(): gathered = lax.all_gather(snapshots, 'row', axis=0, tiled=True)  19 us
  transfers between devices with their start and end apart: 5, of which 4 were waited for; matrix products, arithmetic and copies ran while one was open for 29% of the time, Pallas kernels for 0%

commit v1 on v0

--- a/solution.py
+++ b/solution.py
@@ -1,3 +1,4 @@
+import functools
 import jax
 import jax.numpy as jnp
 from jax import lax
@@ -7,6 +8,13 @@
 SNAPS = 128
 ITERS = 2
 half_root = 0.7071067811865476
+
+
+def point_tails(piece_in, axis_name):
+    return jnp.sum(lax.all_gather(piece_in, axis_name), axis=0)
+
+
+copies_follow = functools.partial(point_tails, axis_name="row")
 
 
 def make_some(extended, offset, start, count):
@@ -62,7 +70,7 @@
         )
         mapped = lax.psum(column_terms, "shift")
         local_gram = jnp.dot(mapped, mapped.T, precision=lax.Precision.HIGHEST)
-        gram_matrix = lax.psum(local_gram, "row")
+        gram_matrix = copies_follow(local_gram)
         own_basis = jnp.dot(factor(gram_matrix), mapped, precision=lax.Precision.HIGHEST)
         if sweep + 1 < ITERS:
             basis_rows = lax.all_gather(own_basis, "row", axis=1, tiled=True)

time: 378 us -> 352 us (0.931)
  blocking collectives: 54.6 us -> 28.6 us
    psum x2 -> x0, blocking collectives: 44.7 us -> none  [per_device(): gram_matrix = lax.psum(local_gram, 'row')]
    all_gather x0 -> x2, blocking collectives: none -> 18.7 us  [point_tails(): return jnp.sum(lax.all_gather(piece_in, axis_name), axis=0)]
  transfers between devices with their start and end apart: 5 -> 5, of which waited for: 4 -> 4; matrix products, arithmetic and copies ran while one was open for 29% -> 31% of each run, Pallas kernels for 0% -> 0%
where the time goes in v1:
time: 352 us; the launch traced here: 349 us
  waiting for transfers between devices  112 us (32%)
  other arithmetic  102 us (29%)
  local copies, waits for them, and re-layouts  39.1 us (11%)
  blocking collectives  28.6 us (8%)
  loops' own time  26.2 us (7%)
  matrix products  26 us (7%)
  between operations  14.5 us (4%)
    psum x2, waiting for transfers between devices, per_device(): mapped = lax.psum(column_terms, 'shift')  69.5 us
    sub x24, other arithmetic, make_some(): difference = window - mirror  28.7 us
    another operation x1, loops' own time, per_device(): lax.fori_loop(0, every_offset.shape[0], add_block, jnp.zeros((block_rows,...  26.2 us
    convert_element_type x24, other arithmetic, make_some(): lax.dynamic_slice_in_dim(extended, offset + M - start - count, count, 0)  26 us
    all_gather x1, waiting for transfers between devices, per_device(): basis_rows = lax.all_gather(own_basis, 'row', axis=1, tiled=True)  22.3 us
    while x120, local copies, waits for them, and re-layouts  19.4 us
    all_gather x1, waiting for transfers between devices, per_device(): gathered = lax.all_gather(snapshots, 'row', axis=0, tiled=True)  19 us
    all_gather x2, blocking collectives, point_tails(): return jnp.sum(lax.all_gather(piece_in, axis_name), axis=0)  18.7 us
  transfers between devices with their start and end apart: 5, of which 4 were waited for; matrix products, arithmetic and copies ran while one was open for 31% of the time, Pallas kernels for 0%

profile of v1, /device:TPU:0, one launch (start us, length us, event | category | flops | bytes accessed | tf_op | source)
XLA Modules:
  0.0 349.4 jit_solution(7911888086102522323)
XLA Ops:
  8.7 1.3 dynamic-slice
  11.5 9.9 %all-reduce = s32[12]{0:T(128)S(1)} all-reduce(s32[12]{0:T(128)S(1)} %dynamic-update-slice.2), channel_id=1, replica_groups=mesh['row'=8,'shift'=4] {'shift'}, use_global_device_ids=true, to_apply=%add | all-reduce | flops 12 | bytes 96
  21.4 19.0 %all-gather.6.cloned.1.call-done = bf16[4096,2,128]{2,1,0:T(2,128)(2,1)} async-done(((bf16[512,2,128]{2,1,0:T(2,128)(2,1)}), bf16[4096,2,128]{2,1,0:T(2,128)(2,1)}) %all-gather.6.cloned.1.call-update) | async-done | bytes 2097168 | tf_op jit(solution)/shard_map/all_gather | solution.py:46
  40.4 6.4 %pad_maximum_fusion = bf16[4224,2,128]{2,1,0:T(2,128)(2,1)S(1)} fusion(bf16[128,2,128]{2,1,0:T(2,128)(2,1)} %param.10, bf16[4096,2,128]{2,1,0:T(2,128)(2,1)} %all-gather.6.cloned.1.call-done), kind=kLoop, calls=%fused_computation.31 | loop fusion | flops 1081344 | bytes 4325376 | tf_op jit(solution)/shard_map/concatenate | solution.py:47
  46.8 1.6 copy.26
  48.4 143.1 %while.18 = (s32[]{:T(128)}, f32[512,1024]{1,0:T(8,128)}, s32[]{:T(128)}, s32[12]{0:T(128)S(1)}, bf16[4224,2,128]{2,0,1:T(8,128)(2,1)}, /*index=5*/s32[]{:T(128)...) while((s32[]{:T(128)}, f32[512,1024]{1,0:T(8,128)}, ...), condition=%wide.region_1.2_spmd.clone, body=%wide.region_0.1_spmd.clone.sunk | while | flops 273222688 | bytes 47713820 | solution.py:60
  52.0 1.2 convert_subtract_fusion.4
  53.2 1.2 slice_bitcast_fusion.8
  59.1 1.3 copy-done.1
  63.9 1.2 convert_subtract_fusion.4
  71.0 1.3 copy-done.1
  75.8 1.2 convert_subtract_fusion.4
  77.1 1.2 slice_bitcast_fusion.8
  82.9 1.3 copy-done.1
  87.8 1.2 convert_subtract_fusion.4
  94.9 1.3 copy-done.1
  99.7 1.2 convert_subtract_fusion.4
  106.8 1.3 copy-done.1
  111.6 1.2 convert_subtract_fusion.4
  118.7 1.3 copy-done.1
  123.5 1.2 convert_subtract_fusion.4
  130.6 1.3 copy-done.1
  135.5 1.2 convert_subtract_fusion.4
  142.6 1.3 copy-done.1
  147.4 1.2 convert_subtract_fusion.4
  154.5 1.3 copy-done.1
  159.3 1.2 convert_subtract_fusion.4
  166.4 1.3 copy-done.1
  171.2 1.2 convert_subtract_fusion.4
  178.3 1.3 copy-done.1
  183.2 1.2 convert_subtract_fusion.4
  190.3 1.3 copy-done.1
  191.6 1.8 broadcast_multiply_fusion
  193.4 4.0 %fusion.16 = f32[64,512]{1,0:T(8,128)} fusion(f32[512,1024]{1,0:T(8,128)S(1)} %broadcast_multiply_fusion, f32[64,4096]{1,0:T(8,128)} %all-gather.8.cloned.1.call-done, s32[]{:T(128)S(6)} %select_n.96), kind=kOutput, calls=%fused_computation.35 | convolution fusion | flops 402653184 | bytes 2490372 | tf_op jit(solution)/shard_map/dot_general | solution.py:68
  197.5 34.7 %all-reduce.4.cloned.1.call-done = f32[64,512]{1,0:T(8,128)} async-done(((f32[64,512]{1,0:T(8,128)}), f32[64,512]{1,0:T(8,128)}) %all-reduce.4.cloned.1.call-update) | async-done | bytes 131088 | tf_op jit(solution)/shard_map/psum | solution.py:71
  232.2 1.2 fusion.32
  233.4 9.2 %all-gather = f32[512,64]{1,0:T(8,128)S(1)} all-gather(f32[64,64]{1,0:T(8,128)S(1)} %fusion.32), channel_id=2, replica_groups=mesh['row'=8,'shift'=4] {'row'}, dimensions={0}, use_global_device_ids=true | all-gather | bytes 147456 | tf_op jit(solution)/shard_map/all_gather | solution.py:14
  242.8 5.8 %cholesky.44 = f32[64,64]{1,0:T(8,128)S(1)} custom-call(f32[64,64]{1,0:T(8,128)S(1)} %fusion.27), custom_call_target="Cholesky" | custom-call | tf_op jit(solution)/shard_map/jit(cholesky)/cholesky | solution.py:35
  250.0 4.9 %custom-call.7 = f32[1,64,64]{1,2,0:T(8,128)S(1)} custom-call(f32[1,64,64]{2,1,0:T(8,128)S(1)} %fusion.22), custom_call_target="InvertDiagBlocksLowerTriangular" | custom-call | tf_op jit(solution)/shard_map/jit(_solve_triangular)/triangular_solve | solution.py:37
  255.1 1.8 fusion.33
  257.0 22.3 %all-gather.10.cloned.1.call-done = f32[64,4096]{1,0:T(8,128)} async-done(((f32[64,512]{1,0:T(8,128)}), f32[64,4096]{1,0:T(8,128)}) %all-gather.10.cloned.1.call-update) | async-done | bytes 1048592 | tf_op jit(solution)/shard_map/all_gather | solution.py:76
  279.3 3.7 %fusion.14 = f32[64,512]{1,0:T(8,128)} fusion(f32[512,1024]{1,0:T(8,128)S(1)} %broadcast_multiply_fusion, f32[64,4096]{1,0:T(8,128)} %all-gather.10.cloned.1.call-done, s32[]{:T(128)S(6)} %select_n.96), kind=kOutput, calls=%fused_computation.33 | convolution fusion | flops 402653184 | bytes 2490372 | tf_op jit(solution)/shard_map/dot_general | solution.py:68
  283.1 34.8 %all-reduce.6.cloned.1.call-done = f32[64,512]{1,0:T(8,128)} async-done(((f32[64,512]{1,0:T(8,128)}), f32[64,512]{1,0:T(8,128)}) %all-reduce.6.cloned.1.call-update) | async-done | bytes 131088 | tf_op jit(solution)/shard_map/psum | solution.py:71
  317.9 1.2 fusion.34
  319.1 9.4 %all-gather.1 = f32[512,64]{1,0:T(8,128)S(1)} all-gather(f32[64,64]{1,0:T(8,128)S(1)} %fusion.34), channel_id=3, replica_groups=mesh['row'=8,'shift'=4] {'row'}, dimensions={0}, use_global_device_ids=true | all-gather | bytes 147456 | tf_op jit(solution)/shard_map/all_gather | solution.py:14
  328.7 5.8 %cholesky.55 = f32[64,64]{1,0:T(8,128)S(1)} custom-call(f32[64,64]{1,0:T(8,128)S(1)} %fusion.25), custom_call_target="Cholesky" | custom-call | tf_op jit(solution)/shard_map/jit(cholesky)/cholesky | solution.py:35
  335.8 4.9 %custom-call.8 = f32[1,64,64]{1,2,0:T(8,128)S(1)} custom-call(f32[1,64,64]{2,1,0:T(8,128)S(1)} %fusion.23), custom_call_target="InvertDiagBlocksLowerTriangular" | custom-call | tf_op jit(solution)/shard_map/jit(_solve_triangular)/triangular_solve | solution.py:37
  341.0 1.8 fusion.35
  (268 shorter events, 89.9 us)
Async XLA Ops:
  7.2 33.2 %all-gather.6.cloned.1.call-start = ((), (), s32[]{:S(2)}) async-start(), calls=%async_computation | async-start | bytes 2359296 | tf_op jit(solution)/shard_map/all_gather | solution.py:46
  7.9 185.5 %all-gather.8.cloned.1.call-start = ((), (), s32[]{:S(2)}) async-start(), calls=%async_computation.1 | async-start | bytes 1179648 | tf_op jit(solution)/shard_map/all_gather | solution.py:64
  8.6 223.5 %all-reduce.4.cloned.1.call-start = ((), (), s32[]{:S(2)}) async-start(), calls=%async_computation.2 | async-start | bytes 262144 | tf_op jit(solution)/shard_map/psum | solution.py:71
  55.7 2.1 copy-start
  56.5 1.4 copy-start.3
  56.5 1.6 copy-start.4
  59.1 1.3 copy-start.1
  67.6 2.1 copy-start
  68.4 1.4 copy-start.3
  68.4 1.6 copy-start.4
  71.0 1.3 copy-start.1
  79.5 2.1 copy-start
  80.4 1.4 copy-start.3
  80.4 1.6 copy-start.4
  82.9 1.3 copy-start.1
  91.5 2.1 copy-start
  92.3 1.4 copy-start.3
  92.3 1.6 copy-start.4
  94.8 1.3 copy-start.1
  103.4 2.1 copy-start
  104.2 1.4 copy-start.3
  104.2 1.6 copy-start.4
  106.8 1.3 copy-start.1
  115.3 2.1 copy-start
  116.1 1.4 copy-start.3
  116.1 1.6 copy-start.4
  118.7 1.3 copy-start.1
  127.2 2.1 copy-start
  128.1 1.4 copy-start.3
  128.1 1.6 copy-start.4
  139.2 2.1 copy-start
  140.0 1.4 copy-start.3
  140.0 1.6 copy-start.4
  151.1 2.1 copy-start
  151.9 1.4 copy-start.3
  151.9 1.6 copy-start.4
  163.0 2.1 copy-start
  163.8 1.4 copy-start.3
  163.8 1.6 copy-start.4
  174.9 2.1 copy-start
  175.8 1.4 copy-start.3
  175.8 1.6 copy-start.4
  186.9 2.1 copy-start
  187.7 1.4 copy-start.3
  187.7 1.6 copy-start.4
  193.4 85.9 %copy-start.5 = (f32[512,1024]{1,0:T(8,128)}, f32[512,1024]{1,0:T(8,128)S(1)}, u32[]{:S(2)}) copy-start(f32[512,1024]{1,0:T(8,128)S(1)} %broadcast_multiply_fusion) | copy-start | bytes 6291460
  197.4 81.9 %all-gather.10.cloned.1.call-start = ((), (), s32[]{:S(2)}) async-start(), calls=%async_computation.3 | async-start | bytes 1179648 | tf_op jit(solution)/shard_map/all_gather | solution.py:76
  257.0 60.9 %all-reduce.6.cloned.1.call-start = ((), (), s32[]{:S(2)}) async-start(), calls=%async_computation.4 | async-start | bytes 262144 | tf_op jit(solution)/shard_map/psum | solution.py:71
  (18 other events, 23.6 us)
Sparse Core Ops, SparseCore 0:
  9.9 30.4 all-gather.5
  42.3 23.3 all-gather.7
  197.5 34.6 all-reduce.3
  257.1 22.1 all-gather.9
  283.2 34.6 all-reduce.5
